TPU v7x, 256 devices: a whole 4x4x8 slice. The times are simulated.
256 devices in a mesh: strip: 256 (over x, z, y, core).
Axes of the slice: x: 4, y: 4, z: 8, core: 2. Of those that a mesh axis runs over, the one named last changes fastest.
Arguments:
- features: bfloat16 [64, 8192, 1024], P(None, 'strip'), may hold values from -6 to 6
- row_kernel: bfloat16 [8, 8, 8, 129], replicated, may hold values from -0.1875 to 0.1875
- mix_weight: bfloat16 [64, 64], replicated, may hold values from -0.75 to 0.75
- channel_bias: float32 [64], replicated, may hold values from -3 to 3
Outputs:
- layer_out: bfloat16 [64, 8192, 1024], P(None, 'strip')
All inputs are finite; a program needn't handle non-finite values.
Results may differ from a plain program's by a relative error of at most 0.001.
Values may be sent and summed in bfloat16 or wider, within the bound.
A program may use at most 128 MiB of HBM per device.

v0:
```python
import jax
import jax.numpy as jnp
from jax import lax
from jax.sharding import PartitionSpec as P


def passed_along(block, axis, distance):
    devices = range(lax.axis_size(axis))
    route = [((i - distance) % len(devices), i) for i in devices]
    return lax.ppermute(block, axis, route)


def local(features, row_kernel, mix_weight, channel_bias):
    channels, strip_rows, columns = features.shape
    group_count, group_width, _, tap_count = row_kernel.shape
    reach = (tap_count - 1) // 2
    strips_away = reach // strip_rows
    above_list = [
        passed_along(features, "strip", distance) for distance in range(strips_away, 0, -1)
    ]
    below_list = [
        passed_along(features, "strip", -distance) for distance in range(1, strips_away + 1)
    ]
    above = jnp.concatenate(above_list, axis=1)
    below = jnp.concatenate(below_list, axis=1)
    ext_rows = strip_rows + 2 * reach
    out_index = lax.broadcasted_iota(jnp.int32, (strip_rows, ext_rows, tap_count), 0)
    in_index = lax.broadcasted_iota(jnp.int32, (strip_rows, ext_rows, tap_count), 1)
    tap_index = lax.broadcasted_iota(jnp.int32, (strip_rows, ext_rows, tap_count), 2)
    one_hot = (in_index - out_index == tap_index).astype(jnp.float32)
    banded = jnp.einsum("goct,pit->gopci", row_kernel.astype(jnp.float32), one_hot).astype(
        jnp.bfloat16
    )
    out_width = group_width * strip_rows
    joined = jnp.concatenate([above, features, below], axis=1)
    span = joined.shape[1]
    matrix = banded.reshape(group_count, out_width, group_width * span)
    data = joined.reshape(group_count, group_width * span, columns)
    conv = jnp.einsum("gab,gbw->gaw", matrix, data, preferred_element_type=jnp.float32)
    conv = conv.reshape(channels, strip_rows, columns)
    mixed = jnp.einsum("io,irw->orw", mix_weight, features, preferred_element_type=jnp.float32)
    total = conv + mixed + channel_bias[:, None, None]
    return jax.nn.gelu(total).astype(jnp.bfloat16)


def solution(mesh):
    return jax.shard_map(
        local,
        mesh=mesh,
        in_specs=(P(None, "strip", None), P(), P(), P()),
        out_specs=P(None, "strip", None),
        check_vma=False,
    )
```

profile of v0, /device:TPU:0, one launch (start us, length us, event | category | flops | bytes accessed | tf_op | source)
XLA Modules:
  0.0 195.9 jit_solution(12046841574717847914)
XLA Ops:
  0.0 0.0 copy-start
  0.0 0.0 collective-permute-start
  0.0 0.0 collective-permute-start.1
  0.0 8.4 %collective-permute-start.2 = (bf16[64,32,1024]{2,1,0:T(8,128)(2,1)}, bf16[64,32,1024]{2,1,0:T(8,128)(2,1)}, u32[]{:S(2)}, u32[]{:S(2)}) collective-permute-start(bf16[64,32,1024]{2,1,0:T(8,128)(2,1)} %param.4), channel_id=1, source_target_pairs={{1,0},{2,1},{3,2},{4,3},{5,4},{6,5},{7,6},{8,7},{9,8},{10,9},{11,1... | collective-permute-start | bytes 12582920 | tf_op jit(solution)/shard_map/ppermute | solution.py:10
  8.4 2.2 %collective-permute-start.3 = (bf16[64,32,1024]{2,1,0:T(8,128)(2,1)}, bf16[64,32,1024]{2,1,0:T(8,128)(2,1)}, u32[]{:S(2)}, u32[]{:S(2)}) collective-permute-start(bf16[64,32,1024]{2,1,0:T(8,128)(2,1)} %param.4), channel_id=1, source_target_pairs={{2,0},{3,1},{4,2},{5,3},{6,4},{7,5},{8,6},{9,7},{10,8},{11,9},{12,... | collective-permute-start | bytes 12582920 | tf_op jit(solution)/shard_map/ppermute | solution.py:10
  10.6 0.0 copy-done
  10.6 5.6 %convert_bitcast_fusion = bf16[8,8,32,8,160]{4,3,1,0,2:T(8,128)(2,1)} fusion(bf16[8,8,8,129]{3,2,1,0:T(8,128)(2,1)S(1)} %copy-done), kind=kOutput, calls=%fused_computation.11 | convolution fusion | flops 680273920 | bytes 5374976 | tf_op jit(solution)/shard_map/goct,pit->gopci/dot_general | solution.py:31
  16.3 7.7 %copy.9 = bf16[8,8,32,8,160]{4,3,2,1,0:T(8,128)(2,1)} copy(bf16[8,8,32,8,160]{4,3,1,0,2:T(8,128)(2,1)} %convert_bitcast_fusion) | data formatting | bytes 10485760 | tf_op jit(solution)/shard_map/convert_element_type | solution.py:31
  24.0 14.2 %reshape.10 = bf16[8,256,1280]{2,1,0:T(8,128)(2,1)} reshape(bf16[8,8,32,8,160]{4,3,2,1,0:T(8,128)(2,1)} %copy.9) | data formatting | bytes 10485760 | tf_op jit(solution)/shard_map/reshape | solution.py:37
  38.2 0.0 copy-start.2
  38.2 62.4 %collective-permute-done = bf16[64,32,1024]{2,1,0:T(8,128)(2,1)} collective-permute-done((bf16[64,32,1024]{2,1,0:T(8,128)(2,1)}, bf16[64,32,1024]{2,1,0:T(8,128)(2,1)}, u32[]{:S(2)}, u32[]{:S(2)}) %collective-permute-start) | collective-permute-done | bytes 4194336 | tf_op jit(solution)/shard_map/ppermute | solution.py:10
  100.5 5.0 %constant_dynamic-update-slice_fusion.4 = bf16[64,160,1024]{2,1,0:T(8,128)(2,1)} fusion(bf16[64,32,1024]{2,1,0:T(8,128)(2,1)} %collective-permute-done), kind=kLoop, calls=%fused_computation.22 | loop fusion | bytes 8388608
  105.6 39.1 %collective-permute-done.1 = bf16[64,32,1024]{2,1,0:T(8,128)(2,1)} collective-permute-done((bf16[64,32,1024]{2,1,0:T(8,128)(2,1)}, bf16[64,32,1024]{2,1,0:T(8,128)(2,1)}, u32[]{:S(2)}, u32[]{:S(2)}) %collective-permute-start.1) | collective-permute-done | bytes 4194336 | tf_op jit(solution)/shard_map/ppermute | solution.py:10
  144.6 5.2 %constant_dynamic-update-slice_fusion.3 = bf16[64,160,1024]{2,1,0:T(8,128)(2,1)} fusion(bf16[64,160,1024]{2,1,0:T(8,128)(2,1)} %constant_dynamic-update-slice_fusion.4, bf16[64,32,1024]{2,1,0:T(8,128)(2,1)} %collective-permute-done.1), kind=kLoop, calls=%fused_computation.21 | loop fusion | bytes 8388608
  149.8 0.0 copy-done.2
  149.8 2.4 %constant_dynamic-update-slice_fusion.2 = bf16[64,160,1024]{2,1,0:T(8,128)(2,1)} fusion(bf16[64,160,1024]{2,1,0:T(8,128)(2,1)} %constant_dynamic-update-slice_fusion.3, bf16[64,32,1024]{2,1,0:T(8,128)(2,1)S(1)} %copy-done.2), kind=kLoop, calls=%fused_computation.20 | loop fusion | bytes 8388608
  152.2 0.0 slice-start
  152.2 0.0 collective-permute-done.2
  152.2 5.2 %constant_dynamic-update-slice_fusion.1 = bf16[64,160,1024]{2,1,0:T(8,128)(2,1)} fusion(bf16[64,160,1024]{2,1,0:T(8,128)(2,1)} %constant_dynamic-update-slice_fusion.2, bf16[64,32,1024]{2,1,0:T(8,128)(2,1)} %collective-permute-done.2), kind=kLoop, calls=%fused_computation.19 | loop fusion | bytes 8388608
  157.5 0.0 slice-start.1
  157.5 0.0 collective-permute-done.3
  157.5 5.2 %constant_dynamic-update-slice_fusion = bf16[64,160,1024]{2,1,0:T(8,128)(2,1)} fusion(bf16[64,160,1024]{2,1,0:T(8,128)(2,1)} %constant_dynamic-update-slice_fusion.1, bf16[64,32,1024]{2,1,0:T(8,128)(2,1)} %collective-permute-done.3), kind=kLoop, calls=%fused_computation.18 | loop fusion | bytes 8388608 | tf_op jit(solution)/shard_map/concatenate | solution.py:35
  162.6 0.0 slice-done
  162.6 0.0 slice-done.1
  162.6 0.0 copy-start.3
  162.6 0.0 copy-start.4
  162.6 15.0 %fusion.17 = f32[8,256,1024]{2,1,0:T(8,128)} fusion(bf16[8,256,1280]{2,1,0:T(8,128)(2,1)S(1)} %bitcast.20, bf16[8,1280,1024]{2,1,0:T(8,128)(2,1)} %bitcast.4), kind=kOutput, calls=%fused_computation.23 | convolution fusion | flops 5368709120 | bytes 34603008 | tf_op jit(solution)/shard_map/gab,gbw->gaw/dot_general | solution.py:39
  177.6 0.0 copy-done.3
  177.6 0.0 copy-done.4
  177.6 13.9 %fusion.7 = bf16[64,32,1024]{2,0,1:T(8,128)(2,1)S(1)} fusion(f32[64,32,1024]{2,1,0:T(8,128)} %bitcast.21, f32[64]{0:T(128)S(1)} %copy-done.4, bf16[64,32,1024]{2,1,0:T(8,128)(2,1)S(1)} %copy-done.2, bf16[64,64]{1,0:T(8,128)(2,1)S(1)} %copy-done.3), kind=kOutput, calls=%fused_computation.8 | convolution fusion | flops 291504128 | bytes 16785664 | tf_op jit(solution)/shard_map/io,irw->orw/dot_general | solution.py:41
  191.5 4.3 %copy.13 = bf16[64,32,1024]{2,1,0:T(8,128)(2,1)} copy(bf16[64,32,1024]{2,0,1:T(8,128)(2,1)S(1)} %fusion.7) | data formatting | bytes 8388608 | tf_op jit(solution)/shard_map/convert_element_type | solution.py:43
  195.9 0.0 copy-done.1
  (2 shorter events, 0.0 us)
Async XLA Ops:
  0.0 10.6 %copy-start = (bf16[8,8,8,129]{3,2,1,0:T(8,128)(2,1)S(1)}, bf16[8,8,8,129]{3,2,1,0:T(8,128)(2,1)}, u32[]{:S(2)}) copy-start(bf16[8,8,8,129]{3,2,1,0:T(8,128)(2,1)} %param.5) | copy-start | bytes 396292
  0.0 100.5 %collective-permute-start = (bf16[64,32,1024]{2,1,0:T(8,128)(2,1)}, bf16[64,32,1024]{2,1,0:T(8,128)(2,1)}, u32[]{:S(2)}, u32[]{:S(2)}) collective-permute-start(bf16[64,32,1024]{2,1,0:T(8,128)(2,1)} %param.4), channel_id=1, source_target_pairs={{254,0},{255,1},{0,2},{1,3},{2,4},{3,5},{4,6},{5,7},{6,8},{7,9},{8... | collective-permute-start | bytes 12582920 | tf_op jit(solution)/shard_map/ppermute | solution.py:10
  0.0 144.6 %collective-permute-start.1 = (bf16[64,32,1024]{2,1,0:T(8,128)(2,1)}, bf16[64,32,1024]{2,1,0:T(8,128)(2,1)}, u32[]{:S(2)}, u32[]{:S(2)}) collective-permute-start(bf16[64,32,1024]{2,1,0:T(8,128)(2,1)} %param.4), channel_id=1, source_target_pairs={{255,0},{0,1},{1,2},{2,3},{3,4},{4,5},{5,6},{6,7},{7,8},{8,9},{9,1... | collective-permute-start | bytes 12582920 | tf_op jit(solution)/shard_map/ppermute | solution.py:10
  0.0 152.2 %collective-permute-start.2 = (bf16[64,32,1024]{2,1,0:T(8,128)(2,1)}, bf16[64,32,1024]{2,1,0:T(8,128)(2,1)}, u32[]{:S(2)}, u32[]{:S(2)}) collective-permute-start(bf16[64,32,1024]{2,1,0:T(8,128)(2,1)} %param.4), channel_id=1, source_target_pairs={{1,0},{2,1},{3,2},{4,3},{5,4},{6,5},{7,6},{8,7},{9,8},{10,9},{11,1... | collective-permute-start | bytes 12582920 | tf_op jit(solution)/shard_map/ppermute | solution.py:10
  8.4 149.1 %collective-permute-start.3 = (bf16[64,32,1024]{2,1,0:T(8,128)(2,1)}, bf16[64,32,1024]{2,1,0:T(8,128)(2,1)}, u32[]{:S(2)}, u32[]{:S(2)}) collective-permute-start(bf16[64,32,1024]{2,1,0:T(8,128)(2,1)} %param.4), channel_id=1, source_target_pairs={{2,0},{3,1},{4,2},{5,3},{6,4},{7,5},{8,6},{9,7},{10,8},{11,9},{12,... | collective-permute-start | bytes 12582920 | tf_op jit(solution)/shard_map/ppermute | solution.py:10
  38.2 111.6 %copy-start.2 = (bf16[64,32,1024]{2,1,0:T(8,128)(2,1)S(1)}, bf16[64,32,1024]{2,1,0:T(8,128)(2,1)}, u32[]{:S(2)}) copy-start(bf16[64,32,1024]{2,1,0:T(8,128)(2,1)} %param.4) | copy-start | bytes 12582916
  152.2 10.4 %slice-start = ((s8[5242880]{0:T(1024)(128)(4,1)}), s8[4194304]{0:T(1024)(128)(4,1)S(1)}, s32[]{:S(2)}) async-start(s8[5242880]{0:T(1024)(128)(4,1)} %bitcast.19), calls=%async_computation | async-start | bytes 8388608
  157.5 5.2 %slice-start.1 = ((s8[5242880]{0:T(1024)(128)(4,1)}), s8[1048576]{0:T(1024)(128)(4,1)S(1)}, s32[]{:S(2)}) async-start(s8[5242880]{0:T(1024)(128)(4,1)} %bitcast.19), calls=%async_computation.1 | async-start | bytes 2097152
  162.6 15.0 %copy-start.3 = (bf16[64,64]{1,0:T(8,128)(2,1)S(1)}, bf16[64,64]{1,0:T(8,128)(2,1)}, u32[]{:S(2)}) copy-start(bf16[64,64]{1,0:T(8,128)(2,1)} %param.6) | copy-start | bytes 24580
  162.6 15.0 %copy-start.4 = (f32[64]{0:T(128)S(1)}, f32[64]{0:T(128)}, u32[]{:S(2)}) copy-start(f32[64]{0:T(128)} %param.7) | copy-start | bytes 772
  177.6 18.2 %copy-start.1 = (bf16[8,8,8,129]{3,2,1,0:T(8,128)(2,1)S(1)}, bf16[8,8,8,129]{3,2,1,0:T(8,128)(2,1)}, u32[]{:S(2)}) copy-start(bf16[8,8,8,129]{3,2,1,0:T(8,128)(2,1)} %param.5) | copy-start | bytes 396292
where the time goes:
time: 196 us
  waiting for transfers between devices  101 us (52%)
  local copies, waits for them, and re-layouts  49.3 us (25%)
  matrix products  34.5 us (18%)
  starting transfers between devices  10.6 us (5%)
    ppermute x4, waiting for transfers between devices, passed_along(): return lax.ppermute(block, axis, route)  101 us
    unnamed x18, local copies, waits for them, and re-layouts  17.9 us
    dot_general x1, matrix products, local(): jnp.einsum('gab,gbw->gaw', matrix, data, preferred_element_type=jnp.float32)  15 us
    reshape x1, local copies, waits for them, and re-layouts, local(): matrix = banded.reshape(group_count, out_width, group_width * span)  14.2 us
    dot_general x1, matrix products, local(): jnp.einsum('io,irw->orw', mix_weight, features, preferred_element_type=jn...  13.9 us
    ppermute x4, starting transfers between devices, passed_along(): return lax.ppermute(block, axis, route)  10.6 us
    convert_element_type x1, local copies, waits for them, and re-layouts, local(): jnp.einsum('goct,pit->gopci', row_kernel.astype(jnp.float32), one_hot)  7.73 us
    dot_general x1, matrix products, local(): jnp.einsum('goct,pit->gopci', row_kernel.astype(jnp.float32), one_hot)  5.63 us
  transfers between devices with their start and end apart: 4, of which 2 were waited for; matrix products, arithmetic and copies ran while one was open for 23% of the time, Pallas kernels for 0%

commit v1 on v0

v1 whole, which is shorter than its diff:
```python
import functools

import jax
import jax.numpy as jnp
from jax import lax
from jax.experimental import pallas as pl
from jax.experimental.pallas import tpu as pltpu
from jax.sharding import PartitionSpec as P

MESH = pl.DeviceIdType.MESH
LANES = 128
TAIL = 4


def kernel(
    n,
    feat,
    taps_in,
    mix_in,
    bias,
    out,
    x,
    taps_raw,
    taps,
    mix,
    band,
    kron,
    spread,
    mixed,
    local_sem,
    own_sem,
    up_send,
    up_recv,
    down_send,
    down_recv,
    side_send,
    side_recv,
    pass_send,
    pass_recv,
):
    channels, strip, columns = feat.shape
    groups, width, _, tap_count = taps_in.shape
    strips = x.shape[1]
    me = lax.axis_index("strip")
    core = lax.rem(me, 2)
    partner = me + 1 - 2 * core
    ahead, behind = lax.rem(me + 2, n), lax.rem(me + n - 2, n)

    def own_copy(g):
        rows = pl.ds(g * width, width)
        return pltpu.make_async_copy(feat.at[rows], x.at[rows, 2], own_sem.at[g])

    for g in range(groups):
        own_copy(g).start()
    small = [
        pltpu.make_async_copy(taps_in, taps_raw, local_sem.at[0]),
        pltpu.make_async_copy(mix_in, mix, local_sem.at[1]),
    ]
    for copy in small:
        copy.start()

    barrier = pltpu.get_barrier_semaphore()
    for device in (ahead, behind, partner):
        pl.semaphore_signal(barrier, inc=1, device_id=(device,), device_id_type=MESH)
    pl.semaphore_wait(barrier, 3)

    wide = [(g * width, 0, columns, g) for g in range(groups - 1)]
    piece = columns // TAIL
    tail = [((groups - 1) * width, q * piece, piece, groups - 1 + q) for q in range(TAIL)]

    def remote(part, source, target, send, recv, device):
        first, column, size, slot = part
        rows, cols = pl.ds(first, width), pl.ds(column, size)
        return pltpu.make_async_remote_copy(
            src_ref=x.at[rows, source, :, cols],
            dst_ref=x.at[rows, target, :, cols],
            send_sem=send.at[slot],
            recv_sem=recv.at[slot],
            device_id=(device,),
            device_id_type=MESH,
        )

    def up(part):
        return remote(part, 2, 0, up_send, up_recv, ahead)

    def down(part):
        return remote(part, 2, 4, down_send, down_recv, behind)

    def side(part):
        return remote(part, 2, 1 + 2 * core, side_send, side_recv, partner)

    def passed(part):
        return remote(part, 4 - 4 * core, 3 - 2 * core, pass_send, pass_recv, partner)

    for part in wide + tail:
        if part[1] == 0:
            own_copy(part[3]).wait()
        up(part).start()
        down(part).start()
        side(part).start()

    for copy in small:
        copy.wait()
    taps[...] = jnp.zeros_like(taps)
    taps[:, :, :, 0:tap_count] = taps_raw[...].astype(jnp.float32)
    spread_channel = lax.broadcasted_iota(jnp.int32, spread.shape, 0)
    spread_column = lax.broadcasted_iota(jnp.int32, spread.shape, 1)
    spread[...] = jnp.where(spread_column // strip == spread_channel, 1.0, 0.0).astype(spread.dtype)

    span = strips * strip
    rows_out = width * strip
    period = taps.shape[-1]

    def build(g):
        for o in range(width):
            tiles = [None] * (width * span // LANES)
            for i in range(width):
                row = taps[g, o, pl.ds(i, 1), :]
                start = i * span
                rolled = pltpu.roll(
                    jnp.broadcast_to(row, (strip, period)),
                    start % LANES,
                    1,
                    stride=1,
                    stride_axis=0,
                )
                for half in range(period // LANES):
                    at = start // LANES + half
                    block = rolled[:, half * LANES : (half + 1) * LANES]
                    if at < len(tiles):
                        tiles[at] = block if tiles[at] is None else tiles[at] + block
            for at, block in enumerate(tiles):
                band[pl.ds(o * strip, strip), pl.ds(at * LANES, LANES)] = block.astype(band.dtype)
        out_row = lax.broadcasted_iota(jnp.int32, (rows_out, channels), 0)
        out_channel = lax.broadcasted_iota(jnp.int32, (rows_out, channels), 1)
        pick = jnp.where(out_row // strip + g * width == out_channel, 1.0, 0.0).astype(mix.dtype)
        picked = lax.dot_general(
            pick, mix[...], (((1,), (1,)), ((), ())), preferred_element_type=jnp.float32
        ).astype(mix.dtype)
        step = 2 * LANES
        for c in range(0, channels * strip, step):
            full = jnp.dot(picked, spread[:, c : c + step], preferred_element_type=jnp.float32)
            p = lax.broadcasted_iota(jnp.int32, full.shape, 0) % strip
            t = lax.broadcasted_iota(jnp.int32, full.shape, 1) % strip
            kron[:, c : c + step] = jnp.where(p == t, full, 0.0).astype(kron.dtype)

        @pl.loop(0, columns // piece)
        def _(q):
            cols = pl.ds(pl.multiple_of(q * piece, piece), piece)
            data = x[:, 2, :, cols].reshape(channels * strip, piece)
            mixed[:, cols] = jnp.dot(kron[...], data, preferred_element_type=jnp.float32)

    def finish(g, cols):
        data = x[pl.ds(g * width, width), :, :, cols].reshape(width * span, piece)
        conv = jnp.dot(band[...], data, preferred_element_type=jnp.float32)
        total = conv + mixed[:, cols]
        for o in range(width):
            c = g * width + o
            value = jax.nn.gelu(total[o * strip : (o + 1) * strip] + bias[c])
            out[c, :, cols] = value.astype(out.dtype)

    @pl.loop(0, groups - 1)
    def _(g):
        build(g)
        part = (g * width, 0, columns, g)
        up(part).wait_recv()
        down(part).wait_recv()
        passed(part).start()
        side(part).wait_recv()
        passed(part).wait_recv()

        @pl.loop(0, columns // piece)
        def _(q):
            finish(g, pl.ds(pl.multiple_of(q * piece, piece), piece))

    last = groups - 1
    build(last)
    for q, part in enumerate(tail):
        up(part).wait_recv()
        down(part).wait_recv()
        passed(part).start()
        if q > 0:
            side(tail[q - 1]).wait_recv()
            passed(tail[q - 1]).wait_recv()
            finish(last, pl.ds((q - 1) * piece, piece))
    side(tail[-1]).wait_recv()
    passed(tail[-1]).wait_recv()
    finish(last, pl.ds((TAIL - 1) * piece, piece))

    for part in wide + tail:
        up(part).wait_send()
        down(part).wait_send()
        side(part).wait_send()
        passed(part).wait_send()


def local(n, features, row_kernel, mix_weight, channel_bias):
    channels, strip, columns = features.shape
    groups, width, _, tap_count = row_kernel.shape
    strips = (tap_count - 1) // strip + 1
    period = -(-(strips * strip + 3 * strip) // LANES) * LANES
    slots = groups - 1 + TAIL
    hbm = pl.BlockSpec(memory_space=pl.ANY)
    return pl.pallas_call(
        functools.partial(kernel, n),
        out_shape=jax.ShapeDtypeStruct(features.shape, jnp.bfloat16),
        in_specs=[hbm, hbm, hbm, pl.BlockSpec(memory_space=pltpu.SMEM)],
        out_specs=pl.BlockSpec(memory_space=pltpu.VMEM),
        scratch_shapes=[
            pltpu.VMEM((channels, strips, strip, columns), jnp.bfloat16),
            pltpu.VMEM(row_kernel.shape, jnp.bfloat16),
            pltpu.VMEM((groups, width, width, period), jnp.float32),
            pltpu.VMEM(mix_weight.shape, jnp.bfloat16),
            pltpu.VMEM((width * strip, width * strips * strip), jnp.bfloat16),
            pltpu.VMEM((width * strip, channels * strip), jnp.bfloat16),
            pltpu.VMEM((channels, channels * strip), jnp.bfloat16),
            pltpu.VMEM((width * strip, columns), jnp.float32),
            pltpu.SemaphoreType.DMA((2,)),
            pltpu.SemaphoreType.DMA((groups,)),
        ]
        + [pltpu.SemaphoreType.DMA((slots,))] * 8,
        compiler_params=pltpu.CompilerParams(
            collective_id=0, has_side_effects=True, vmem_limit_bytes=48 * 2**20
        ),
    )(features, row_kernel, mix_weight, channel_bias)


def solution(mesh):
    return jax.shard_map(
        functools.partial(local, mesh.shape["strip"]),
        mesh=mesh,
        in_specs=(P(None, "strip", None), P(), P(), P()),
        out_specs=P(None, "strip", None),
        check_vma=False,
    )
```

time: 196 us -> 111 us (0.57)
  the two profiles are of different devices: /device:TPU:0 before, /device:TPU:1 now
where the time goes in v1:
time: 111 us
  Pallas kernels  106 us (95%)
  local copies, waits for them, and re-layouts  4.34 us (4%)
    pallas_call x1, Pallas kernels, local(): pl.pallas_call(functools.partial(kernel, n), out_shape=jax.ShapeDtypeStru...  106 us
    unnamed x7, local copies, waits for them, and re-layouts  4.34 us

profile of v1, /device:TPU:1, one launch (start us, length us, event | category | flops | bytes accessed | tf_op | source)
XLA Modules:
  0.0 110.8 jit_solution(11322058132748854399)
XLA Ops:
  0.0 0.0 copy-start
  0.0 0.9 copy-done
  1.0 0.0 copy-start.1
  1.0 0.7 copy-done.1
  1.7 0.0 copy-start.2
  1.7 0.7 copy-done.2
  2.3 106.5 %shard_map.46 = bf16[64,32,1024]{2,1,0:T(8,128)(2,1)S(1)} custom-call(bf16[64,32,1024]{2,1,0:T(8,128)(2,1)} %feat.1, bf16[8,8,8,129]{3,2,1,0:T(8,128)(2,1)S(1)} %copy-done, bf16[64,64]{1,0:T(8,128)(2,1)S(1)} %copy-done.1, f32[64]{0:T(128)S(1)} %copy-done.2), custom_call_target="tpu_custom_call" | custom-call | tf_op jit(solution)/shard_map/pallas_call | solution.py:204
  108.8 2.0 %copy.6 = bf16[64,32,1024]{2,1,0:T(8,128)(2,1)} copy(bf16[64,32,1024]{2,1,0:T(8,128)(2,1)S(1)} %shard_map.46) | data formatting | bytes 8388608
Async XLA Ops:
  0.0 0.9 copy-start
  1.0 0.7 copy-start.1
  1.7 0.7 copy-start.2

commit v2 on v1

v2 whole, which is shorter than its diff:
```python
import functools

import jax
import jax.numpy as jnp
from jax import lax
from jax.experimental import pallas as pl
from jax.experimental.pallas import tpu as pltpu
from jax.sharding import PartitionSpec as P

MESH = pl.DeviceIdType.MESH
LANES = 128
TAIL = 384, 384, 256
TILE = 512
LEAD = 3
SLAB = 32
LINE = 4


def kernel(
    n,
    feat,
    taps_in,
    mix_in,
    bias_in,
    out,
    x,
    taps_raw,
    taps,
    mix,
    bias,
    band,
    kron,
    spread,
    mixed,
    landing,
    local_sem,
    own_sem,
    flow_send,
    flow_recv,
    side_send,
    side_recv,
    pass_send,
    pass_recv,
    land_send,
    land_recv,
    ready,
):
    channels, strip, columns = feat.shape
    groups, width, _, tap_count = taps_in.shape
    strips = x.shape[1]
    me = lax.axis_index("strip")
    core = lax.rem(me, 2)
    partner = me + 1 - 2 * core
    ahead, behind = lax.rem(me + 2, n), lax.rem(me + n - 2, n)
    place = lax.rem(lax.div(me, 2), SLAB)
    first = (place == 0).astype(jnp.int32)
    last_chip = (place == SLAB - 1).astype(jnp.int32)
    step = 2 * (SLAB - LINE)
    relays_up = (place * 2 == step).astype(jnp.int32)
    relays_down = ((SLAB - 1 - place) * 2 == step).astype(jnp.int32)

    def wrapped(device):
        return lax.rem(device + n, n)

    def own_copy(g):
        rows = pl.ds(g * width, width)
        return pltpu.make_async_copy(feat.at[rows], x.at[rows, 2], own_sem.at[g])

    for g in [groups - 1] + list(range(groups - 1)):
        own_copy(g).start()
    small = [
        pltpu.make_async_copy(taps_in, taps_raw, local_sem.at[0]),
        pltpu.make_async_copy(mix_in, mix, local_sem.at[1]),
        pltpu.make_async_copy(bias_in, bias, local_sem.at[2]),
    ]
    for copy in small:
        copy.start()

    barrier = pltpu.get_barrier_semaphore()

    def greet(device):
        pl.semaphore_signal(barrier, inc=1, device_id=(device,), device_id_type=MESH)

    greet(behind)
    greet(partner)

    @pl.when(last_chip == 0)
    def _():
        greet(ahead)

    @pl.when(first == 1)
    def _():
        greet(me + step)

    @pl.when(relays_up == 1)
    def _():
        greet(wrapped(me - step - 2))

    @pl.when(relays_down == 1)
    def _():
        greet(me + step)
        greet(wrapped(me + step + 2))

    pl.semaphore_wait(barrier, 3 + 2 * last_chip + relays_up)

    @pl.when(last_chip == 1)
    def _():
        for device in (ahead, me - step):
            pl.semaphore_signal(ready, inc=1, device_id=(device,), device_id_type=MESH)

    wide = [(g * width, 0, columns, g) for g in range(groups - 1)]
    last = groups - 1
    tail = [(last * width, sum(TAIL[:q]), size, last + q) for q, size in enumerate(TAIL)]
    relayed = tail[0]

    def block(part, strip_at):
        first_channel, column, size, _ = part
        return x.at[pl.ds(first_channel, width), strip_at, :, pl.ds(column, size)]

    def remote(source, target, send, recv, device):
        return pltpu.make_async_remote_copy(
            src_ref=source,
            dst_ref=target,
            send_sem=send,
            recv_sem=recv,
            device_id=(device,),
            device_id_type=MESH,
        )

    def flow(part, way):
        device = ahead + way * (behind - ahead)
        sems = flow_send.at[way, part[3]], flow_recv.at[way, part[3]]
        return remote(block(part, 2), block(part, 4 * way), *sems, device)

    def side(part):
        sems = side_send.at[part[3]], side_recv.at[part[3]]
        return remote(block(part, 2), block(part, 1 + 2 * core), *sems, partner)

    def passed(part):
        sems = pass_send.at[part[3]], pass_recv.at[part[3]]
        return remote(block(part, 4 - 4 * core), block(part, 3 - 2 * core), *sems, partner)

    def to_relay(way):
        device = wrapped(ahead + step) if way == 0 else wrapped(behind - step)
        return remote(block(relayed, 2), landing, flow_send.at[way, relayed[3]], land_recv, device)

    def from_relay(way):
        target = block(relayed, 4 * way)
        return remote(landing, target, land_send, flow_recv.at[way, relayed[3]], me + (2 * way - 1) * step)

    def start_tail(way):
        @pl.when(last_chip * (1 - way) + first * way == 0)
        def _():
            flow(relayed, way).start()

        for part in tail[1:]:
            flow(part, way).start()

    own_copy(last).wait()
    for to, sender in enumerate((last_chip, first)):

        @pl.when(sender == 1)
        def _():
            to_relay(to).start()

    way = (1 - core) * (1 - first)
    for part in wide[:LEAD]:
        own_copy(part[3]).wait()
        flow(part, way).start()
    for part in wide[:LEAD]:
        side(part).start()
    for part in wide[LEAD:]:
        own_copy(part[3]).wait()

    for copy in small:
        copy.wait()
    taps[...] = jnp.zeros_like(taps)
    taps[:, :, :, 0:tap_count] = taps_raw[...].astype(jnp.float32)
    spread_channel = lax.broadcasted_iota(jnp.int32, spread.shape, 0)
    spread_column = lax.broadcasted_iota(jnp.int32, spread.shape, 1)
    spread[...] = jnp.where(spread_column // strip == spread_channel, 1.0, 0.0).astype(spread.dtype)

    @pl.when(first == 1)
    def _():
        pl.semaphore_wait(ready, 1)

    for part in wide[:LEAD]:
        flow(part, 1 - way).start()

    for to, relays in enumerate((relays_up, relays_down)):

        @pl.when(relays == 1)
        def _():
            if to == 1:
                pl.semaphore_wait(ready, 1)
            to_relay(to).wait_recv()
            from_relay(to).start()

    span = strips * strip
    rows_out = width * strip
    period = taps.shape[-1]

    def build(g):
        for o in range(width):
            tiles = [None] * (width * span // LANES)
            for i in range(width):
                row = taps[g, o, pl.ds(i, 1), :]
                start = i * span
                rolled = pltpu.roll(
                    jnp.broadcast_to(row, (strip, period)),
                    start % LANES,
                    1,
                    stride=1,
                    stride_axis=0,
                )
                for half in range(period // LANES):
                    at = start // LANES + half
                    tile = rolled[:, half * LANES : (half + 1) * LANES]
                    if at < len(tiles):
                        tiles[at] = tile if tiles[at] is None else tiles[at] + tile
            for at, tile in enumerate(tiles):
                band[pl.ds(o * strip, strip), pl.ds(at * LANES, LANES)] = tile.astype(band.dtype)
        out_row = lax.broadcasted_iota(jnp.int32, (rows_out, channels), 0)
        out_channel = lax.broadcasted_iota(jnp.int32, (rows_out, channels), 1)
        pick = jnp.where(out_row // strip + g * width == out_channel, 1.0, 0.0).astype(mix.dtype)
        picked = lax.dot_general(
            pick, mix[...], (((1,), (1,)), ((), ())), preferred_element_type=jnp.float32
        ).astype(mix.dtype)
        step = 2 * LANES
        for c in range(0, channels * strip, step):
            full = jnp.dot(picked, spread[:, c : c + step], preferred_element_type=jnp.float32)
            p = lax.broadcasted_iota(jnp.int32, full.shape, 0) % strip
            t = lax.broadcasted_iota(jnp.int32, full.shape, 1) % strip
            kron[:, c : c + step] = jnp.where(p == t, full, 0.0).astype(kron.dtype)

        @pl.loop(0, columns // TILE)
        def _(q):
            cols = pl.ds(pl.multiple_of(q * TILE, TILE), TILE)
            data = x[:, 2, :, cols].reshape(channels * strip, TILE)
            mixed[:, cols] = jnp.dot(kron[...], data, preferred_element_type=jnp.float32)

    def finish(g, column, size):
        cols = pl.ds(column, size)
        data = x[pl.ds(g * width, width), :, :, cols].reshape(width * span, size)
        conv = jnp.dot(band[...], data, preferred_element_type=jnp.float32)
        total = conv + mixed[:, cols]
        for o in range(width):
            c = g * width + o
            value = jax.nn.gelu(total[o * strip : (o + 1) * strip] + bias[c])
            out[c, :, cols] = value.astype(out.dtype)

    @pl.loop(0, groups - 1)
    def _(g):
        build(g)
        part = (g * width, 0, columns, g)
        flow(part, 0).wait_recv()
        flow(part, 1).wait_recv()
        passed(part).start()

        @pl.when(g + LEAD < groups - 1)
        def _():
            later = ((g + LEAD) * width, 0, columns, g + LEAD)
            flow(later, way).start()
            flow(later, 1 - way).start()
            side(later).start()

        @pl.when(g + LEAD == groups - 1)
        def _():
            start_tail(way)
            start_tail(1 - way)
            for later in tail:
                side(later).start()

        side(part).wait_recv()
        passed(part).wait_recv()

        @pl.loop(0, columns // TILE)
        def _(q):
            finish(g, pl.multiple_of(q * TILE, TILE), TILE)

    build(last)
    for q, part in enumerate(tail):
        flow(part, 0).wait_recv()
        flow(part, 1).wait_recv()
        passed(part).start()
        if q > 0:
            side(tail[q - 1]).wait_recv()
            passed(tail[q - 1]).wait_recv()
            finish(last, *tail[q - 1][1:3])
    side(tail[-1]).wait_recv()
    passed(tail[-1]).wait_recv()
    finish(last, *tail[-1][1:3])

    for part in wide + tail:
        flow(part, 0).wait_send()
        flow(part, 1).wait_send()
        side(part).wait_send()
        passed(part).wait_send()

    @pl.when(relays_up + relays_down == 1)
    def _():
        from_relay(0).wait_send()


def local(n, features, row_kernel, mix_weight, channel_bias):
    channels, strip, columns = features.shape
    groups, width, _, tap_count = row_kernel.shape
    strips = (tap_count - 1) // strip + 1
    period = -(-(strips * strip + 3 * strip) // LANES) * LANES
    slots = groups - 1 + len(TAIL)
    small = row_kernel, mix_weight, channel_bias
    hbm = pl.BlockSpec(memory_space=pltpu.HBM)
    return pl.pallas_call(
        functools.partial(kernel, n),
        out_shape=jax.ShapeDtypeStruct(features.shape, jnp.bfloat16),
        in_specs=[hbm, hbm, hbm, hbm],
        out_specs=pl.BlockSpec(memory_space=pltpu.VMEM),
        scratch_shapes=[
            pltpu.VMEM((channels, strips, strip, columns), jnp.bfloat16),
            pltpu.VMEM(row_kernel.shape, jnp.bfloat16),
            pltpu.VMEM((groups, width, width, period), jnp.float32),
            pltpu.VMEM(mix_weight.shape, jnp.bfloat16),
            pltpu.SMEM(channel_bias.shape, jnp.float32),
            pltpu.VMEM((width * strip, width * strips * strip), jnp.bfloat16),
            pltpu.VMEM((width * strip, channels * strip), jnp.bfloat16),
            pltpu.VMEM((channels, channels * strip), jnp.bfloat16),
            pltpu.VMEM((width * strip, columns), jnp.float32),
            pltpu.VMEM((width, strip, TAIL[0]), jnp.bfloat16),
            pltpu.SemaphoreType.DMA((3,)),
            pltpu.SemaphoreType.DMA((groups,)),
        ]
        + [pltpu.SemaphoreType.DMA((2, slots))] * 2
        + [pltpu.SemaphoreType.DMA((slots,))] * 4
        + [pltpu.SemaphoreType.DMA] * 2
        + [pltpu.SemaphoreType.REGULAR],
        compiler_params=pltpu.CompilerParams(
            collective_id=0, has_side_effects=True, vmem_limit_bytes=48 * 2**20
        ),
    )(features, *(pltpu.with_memory_space_constraint(a, pltpu.HBM) for a in small))


def solution(mesh):
    return jax.shard_map(
        functools.partial(local, mesh.shape["strip"]),
        mesh=mesh,
        in_specs=(P(None, "strip", None), P(), P(), P()),
        out_specs=P(None, "strip", None),
        check_vma=False,
    )
```

time: 111 us -> 106 us (0.955)
  local copies, waits for them, and re-layouts: 4.34 us -> 2.02 us
  Pallas kernels: 106 us -> 104 us
    pallas_call x1, Pallas kernels: 106 us -> 104 us  [local(): pl.pallas_call(functools.partial(kernel, n), out_shape=jax.ShapeDtypeStru...]
    unnamed x7 -> x1, local copies, waits for them, and re-layouts: 4.34 us -> 2.02 us
where the time goes in v2:
time: 106 us
  Pallas kernels  104 us (98%)
  local copies, waits for them, and re-layouts  2.02 us (2%)
    pallas_call x1, Pallas kernels, local(): pl.pallas_call(functools.partial(kernel, n), out_shape=jax.ShapeDtypeStru...  104 us

profile of v2, /device:TPU:1, one launch (start us, length us, event | category | flops | bytes accessed | tf_op | source)
XLA Modules:
  0.0 105.7 jit_solution(3831409948667944022)
XLA Ops:
  0.0 103.7 %shard_map.46 = bf16[64,32,1024]{2,1,0:T(8,128)(2,1)S(1)} custom-call(bf16[64,32,1024]{2,1,0:T(8,128)(2,1)} %feat.1, bf16[8,8,8,129]{3,2,1,0:T(8,128)(2,1)} %taps_in.1, bf16[64,64]{1,0:T(8,128)(2,1)} %mix_in.1, f32[64]{0:T(128)} %bias_in.1), custom_call_target="tpu_custom_call" | custom-call | tf_op jit(solution)/shard_map/pallas_call | solution.py:313
  103.7 2.0 %copy.6 = bf16[64,32,1024]{2,1,0:T(8,128)(2,1)} copy(bf16[64,32,1024]{2,1,0:T(8,128)(2,1)S(1)} %shard_map.46) | data formatting | bytes 8388608

commit v3 on v2

--- a/solution.py
+++ b/solution.py
@@ -9,7 +9,8 @@
 
 MESH = pl.DeviceIdType.MESH
 LANES = 128
-TAIL = 384, 384, 256
+TAIL = 256, 256, 512
+RELAYS = 2
 TILE = 512
 LEAD = 3
 SLAB = 32
@@ -44,6 +45,7 @@
     land_send,
     land_recv,
     ready,
+    settled,
 ):
     channels, strip, columns = feat.shape
     groups, width, _, tap_count = taps_in.shape
@@ -55,9 +57,9 @@
     place = lax.rem(lax.div(me, 2), SLAB)
     first = (place == 0).astype(jnp.int32)
     last_chip = (place == SLAB - 1).astype(jnp.int32)
-    step = 2 * (SLAB - LINE)
-    relays_up = (place * 2 == step).astype(jnp.int32)
-    relays_down = ((SLAB - 1 - place) * 2 == step).astype(jnp.int32)
+    steps = [2 * (SLAB - LINE * (j + 1)) for j in range(RELAYS)]
+    relays_up = [(place * 2 == step).astype(jnp.int32) for step in steps]
+    relays_down = [((SLAB - 1 - place) * 2 == step).astype(jnp.int32) for step in steps]
 
     def wrapped(device):
         return lax.rem(device + n, n)
@@ -88,30 +90,42 @@
     def _():
         greet(ahead)
 
-    @pl.when(first == 1)
-    def _():
-        greet(me + step)
-
-    @pl.when(relays_up == 1)
-    def _():
-        greet(wrapped(me - step - 2))
-
-    @pl.when(relays_down == 1)
-    def _():
-        greet(me + step)
-        greet(wrapped(me + step + 2))
-
-    pl.semaphore_wait(barrier, 3 + 2 * last_chip + relays_up)
+    for j, step in enumerate(steps):
+
+        @pl.when(first == 1)
+        def _():
+            greet(me + step)
+            if j > 0:
+                greet(wrapped(me - step - 2))
+
+        @pl.when(relays_up[j] == 1)
+        def _():
+            greet(wrapped(me - step - 2))
+
+        @pl.when(relays_down[j] == 1)
+        def _():
+            greet(me + step)
+            if j == 0:
+                greet(wrapped(me + step + 2))
+
+    pl.semaphore_wait(barrier, 3 + 2 * RELAYS * last_chip + sum(relays_up) + sum(relays_down[1:]))
 
     @pl.when(last_chip == 1)
     def _():
-        for device in (ahead, me - step):
+        for device in [ahead] + [me - step for step in steps]:
             pl.semaphore_signal(ready, inc=1, device_id=(device,), device_id_type=MESH)
+
+    for j, step in list(enumerate(steps))[1:]:
+
+        @pl.when(relays_down[j] == 1)
+        def _():
+            device = wrapped(me + step + 2)
+            pl.semaphore_signal(settled, inc=1, device_id=(device,), device_id_type=MESH)
 
     wide = [(g * width, 0, columns, g) for g in range(groups - 1)]
     last = groups - 1
     tail = [(last * width, sum(TAIL[:q]), size, last + q) for q, size in enumerate(TAIL)]
-    relayed = tail[0]
+    relayed = tail[:RELAYS]
 
     def block(part, strip_at):
         first_channel, column, size, _ = part
@@ -140,28 +154,35 @@
         sems = pass_send.at[part[3]], pass_recv.at[part[3]]
         return remote(block(part, 4 - 4 * core), block(part, 3 - 2 * core), *sems, partner)
 
-    def to_relay(way):
-        device = wrapped(ahead + step) if way == 0 else wrapped(behind - step)
-        return remote(block(relayed, 2), landing, flow_send.at[way, relayed[3]], land_recv, device)
-
-    def from_relay(way):
-        target = block(relayed, 4 * way)
-        return remote(landing, target, land_send, flow_recv.at[way, relayed[3]], me + (2 * way - 1) * step)
+    def to_relay(way, j):
+        part = relayed[j]
+        device = wrapped(ahead + steps[j]) if way == 0 else wrapped(behind - steps[j])
+        return remote(block(part, 2), landing, flow_send.at[way, part[3]], land_recv, device)
+
+    def from_relay(way, j):
+        part = relayed[j]
+        device = me + (2 * way - 1) * steps[j]
+        return remote(landing, block(part, 4 * way), land_send, flow_recv.at[way, part[3]], device)
 
     def start_tail(way):
         @pl.when(last_chip * (1 - way) + first * way == 0)
         def _():
-            flow(relayed, way).start()
-
-        for part in tail[1:]:
+            for part in relayed:
+                flow(part, way).start()
+
+        for part in tail[RELAYS:]:
             flow(part, way).start()
 
     own_copy(last).wait()
-    for to, sender in enumerate((last_chip, first)):
-
-        @pl.when(sender == 1)
-        def _():
-            to_relay(to).start()
+
+    @pl.when(last_chip == 1)
+    def _():
+        for j in range(RELAYS):
+            to_relay(0, j).start()
+
+    @pl.when(first == 1)
+    def _():
+        to_relay(1, 0).start()
 
     way = (1 - core) * (1 - first)
     for part in wide[:LEAD]:
@@ -172,6 +193,12 @@
     for part in wide[LEAD:]:
         own_copy(part[3]).wait()
 
+    @pl.when(first == 1)
+    def _():
+        pl.semaphore_wait(settled, RELAYS - 1)
+        for j in range(1, RELAYS):
+            to_relay(1, j).start()
+
     for copy in small:
         copy.wait()
     taps[...] = jnp.zeros_like(taps)
@@ -188,13 +215,14 @@
         flow(part, 1 - way).start()
 
     for to, relays in enumerate((relays_up, relays_down)):
-
-        @pl.when(relays == 1)
-        def _():
-            if to == 1:
-                pl.semaphore_wait(ready, 1)
-            to_relay(to).wait_recv()
-            from_relay(to).start()
+        for j in range(RELAYS):
+
+            @pl.when(relays[j] == 1)
+            def _():
+                if to == 1:
+                    pl.semaphore_wait(ready, 1)
+                to_relay(to, j).wait_recv()
+                from_relay(to, j).start()
 
     span = strips * strip
     rows_out = width * strip
@@ -297,9 +325,9 @@
         side(part).wait_send()
         passed(part).wait_send()
 
-    @pl.when(relays_up + relays_down == 1)
-    def _():
-        from_relay(0).wait_send()
+    @pl.when(sum(relays_up) + sum(relays_down) == 1)
+    def _():
+        from_relay(0, 0).wait_send()
 
 
 def local(n, features, row_kernel, mix_weight, channel_bias):
@@ -332,7 +360,7 @@
         + [pltpu.SemaphoreType.DMA((2, slots))] * 2
         + [pltpu.SemaphoreType.DMA((slots,))] * 4
         + [pltpu.SemaphoreType.DMA] * 2
-        + [pltpu.SemaphoreType.REGULAR],
+        + [pltpu.SemaphoreType.REGULAR] * 2,
         compiler_params=pltpu.CompilerParams(
             collective_id=0, has_side_effects=True, vmem_limit_bytes=48 * 2**20
         ),

time: 106 us -> 106 us (level)
  no operation moved by 1% of the time
where the time goes in v3:
time: 106 us
  Pallas kernels  104 us (98%)
  local copies, waits for them, and re-layouts  2.02 us (2%)
    pallas_call x1, Pallas kernels, local(): pl.pallas_call(functools.partial(kernel, n), out_shape=jax.ShapeDtypeStru...  104 us

profile of v3, /device:TPU:1, one launch (start us, length us, event | category | flops | bytes accessed | tf_op | source)
XLA Modules:
  0.0 105.8 jit_solution(13298874278939943785)
XLA Ops:
  0.0 103.7 %shard_map.46 = bf16[64,32,1024]{2,1,0:T(8,128)(2,1)S(1)} custom-call(bf16[64,32,1024]{2,1,0:T(8,128)(2,1)} %feat.1, bf16[8,8,8,129]{3,2,1,0:T(8,128)(2,1)} %taps_in.1, bf16[64,64]{1,0:T(8,128)(2,1)} %mix_in.1, f32[64]{0:T(128)} %bias_in.1), custom_call_target="tpu_custom_call" | custom-call | tf_op jit(solution)/shard_map/pallas_call | solution.py:341
  103.8 2.0 %copy.6 = bf16[64,32,1024]{2,1,0:T(8,128)(2,1)} copy(bf16[64,32,1024]{2,1,0:T(8,128)(2,1)S(1)} %shard_map.46) | data formatting | bytes 8388608

commit v4 on v3

--- a/solution.py
+++ b/solution.py
@@ -9,7 +9,7 @@
 
 MESH = pl.DeviceIdType.MESH
 LANES = 128
-TAIL = 256, 256, 512
+TAIL = 384, 256, 384
 RELAYS = 2
 TILE = 512
 LEAD = 3
@@ -154,15 +154,18 @@
         sems = pass_send.at[part[3]], pass_recv.at[part[3]]
         return remote(block(part, 4 - 4 * core), block(part, 3 - 2 * core), *sems, partner)
 
+    def landed(part):
+        return landing.at[:, :, pl.ds(0, part[2])]
+
     def to_relay(way, j):
         part = relayed[j]
         device = wrapped(ahead + steps[j]) if way == 0 else wrapped(behind - steps[j])
-        return remote(block(part, 2), landing, flow_send.at[way, part[3]], land_recv, device)
+        return remote(block(part, 2), landed(part), flow_send.at[way, part[3]], land_recv, device)
 
     def from_relay(way, j):
         part = relayed[j]
         device = me + (2 * way - 1) * steps[j]
-        return remote(landing, block(part, 4 * way), land_send, flow_recv.at[way, part[3]], device)
+        return remote(landed(part), block(part, 4 * way), land_send, flow_recv.at[way, part[3]], device)
 
     def start_tail(way):
         @pl.when(last_chip * (1 - way) + first * way == 0)
@@ -325,9 +328,11 @@
         side(part).wait_send()
         passed(part).wait_send()
 
-    @pl.when(sum(relays_up) + sum(relays_down) == 1)
-    def _():
-        from_relay(0, 0).wait_send()
+    for j in range(RELAYS):
+
+        @pl.when(relays_up[j] + relays_down[j] == 1)
+        def _():
+            from_relay(0, j).wait_send()
 
 
 def local(n, features, row_kernel, mix_weight, channel_bias):
@@ -353,7 +358,7 @@
             pltpu.VMEM((width * strip, channels * strip), jnp.bfloat16),
             pltpu.VMEM((channels, channels * strip), jnp.bfloat16),
             pltpu.VMEM((width * strip, columns), jnp.float32),
-            pltpu.VMEM((width, strip, TAIL[0]), jnp.bfloat16),
+            pltpu.VMEM((width, strip, max(TAIL[:RELAYS])), jnp.bfloat16),
             pltpu.SemaphoreType.DMA((3,)),
             pltpu.SemaphoreType.DMA((groups,)),
         ]

time: 106 us -> 106 us (level)
  no operation moved by 1% of the time
where the time goes in v4:
time: 106 us
  Pallas kernels  104 us (98%)
  local copies, waits for them, and re-layouts  2.02 us (2%)
    pallas_call x1, Pallas kernels, local(): pl.pallas_call(functools.partial(kernel, n), out_shape=jax.ShapeDtypeStru...  104 us

profile of v4, /device:TPU:1, one launch (start us, length us, event | category | flops | bytes accessed | tf_op | source)
XLA Modules:
  0.0 105.9 jit_solution(15643329770830299199)
XLA Ops:
  0.0 103.8 %shard_map.46 = bf16[64,32,1024]{2,1,0:T(8,128)(2,1)S(1)} custom-call(bf16[64,32,1024]{2,1,0:T(8,128)(2,1)} %feat.1, bf16[8,8,8,129]{3,2,1,0:T(8,128)(2,1)} %taps_in.1, bf16[64,64]{1,0:T(8,128)(2,1)} %mix_in.1, f32[64]{0:T(128)} %bias_in.1), custom_call_target="tpu_custom_call" | custom-call | tf_op jit(solution)/shard_map/pallas_call | solution.py:346
  103.8 2.0 %copy.6 = bf16[64,32,1024]{2,1,0:T(8,128)(2,1)} copy(bf16[64,32,1024]{2,1,0:T(8,128)(2,1)S(1)} %shard_map.46) | data formatting | bytes 8388608
